TPU v7x, 32 devices: a whole 2x2x4 slice. The times are simulated.
32 devices in a mesh: gx: 4 (over x, core), gy: 8 (over z, y).
Axes of the slice: x: 2, y: 2, z: 4, core: 2. Of those that a mesh axis runs over, the one named last changes fastest.
Arguments:
- hot_ids: int32 [262144], P(('gx', 'gy')), may hold values from 0 to 2047
- hot_grads: bfloat16 [262144, 128], P(('gx', 'gy')), may hold values from -6 to 6
- cold_grads: bfloat16 [4, 8, 8, 512, 128], P('gx', 'gy'), may hold values from -6 to 6
- cold_slots: int32 [4, 8, 8, 512], P('gx', 'gy'), may hold values from 0 to 2047
- cold_counts: int32 [4, 8, 8], P('gx', 'gy'), may hold values from 1 to 512, as said below
Outputs:
- hot_grad: float32 [2048, 128], replicated
- cold_grad: float32 [4, 16384, 128], P('gx', 'gy')
Inputs may be any that keep to these rules, and one draw needn't show every extreme that they name: In each group g, some owner d receives cold_counts[g, s, d] = 512 from every s; loads per owner are skewed.
All inputs are finite; a program needn't handle non-finite values.
Results may differ from a plain program's by a relative error of at most 0.0003.
Values may be sent and summed in bfloat16 or wider, within the bound.
A program may use at most 64 MiB of HBM per device.

v0:
```python
import math

import jax
import jax.numpy as jnp
from jax import lax
from jax.sharding import PartitionSpec as P

HOT = 2048
OWN_ROWS = 2048


def onehot_sum(row_ids, row_data, table_size, block_rows):
    turns = row_ids.shape[0] // block_rows
    id_blocks = row_ids.reshape(turns, block_rows)
    data_blocks = row_data.reshape(turns, block_rows, row_data.shape[1])
    table_iota = lax.broadcasted_iota(jnp.int32, (table_size, block_rows), 0)

    def add_block(total, pieces):
        ids_here, data_here = pieces
        selector = (table_iota == ids_here[None, :]).astype(jnp.bfloat16)
        return (total + jnp.dot(selector, data_here, preferred_element_type=jnp.float32), None)

    start = jnp.zeros((table_size, row_data.shape[1]), jnp.float32)
    total, unused = lax.scan(add_block, start, (id_blocks, data_blocks))
    return total


def hot_part(hot_ids, hot_grads):
    hot_rows = HOT
    block_rows = math.gcd(hot_ids.shape[0], 2048)
    local_sum = onehot_sum(hot_ids, hot_grads, hot_rows, block_rows)
    factor = (hot_rows / (hot_ids.shape[0] * lax.axis_size("gx") * lax.axis_size("gy"))) ** 0.5
    shared = lax.psum_scatter(local_sum, "gy", scatter_dimension=0, tiled=True)
    shared = lax.psum(shared, "gx")
    total = lax.all_gather(shared, "gy", axis=0, tiled=True)
    return total * factor


def cold_part(cold_grads, cold_slots, cold_counts):
    owners, capacity, width = (cold_grads.shape[2], cold_grads.shape[3], cold_grads.shape[4])
    grads_here = cold_grads.reshape(owners, capacity, width)
    slots_here = cold_slots.reshape(owners, capacity)
    counts_here = cold_counts.reshape(owners)
    places = lax.broadcasted_iota(jnp.int32, (owners, capacity), 1)
    valid = places < counts_here[:, None]
    payload = jnp.where(valid[:, :, None], grads_here, jnp.zeros_like(grads_here))
    got_rows, got_slots = (
        lax.all_to_all(payload, "gy", split_axis=0, concat_axis=0, tiled=True),
        lax.all_to_all(slots_here, "gy", split_axis=0, concat_axis=0, tiled=True),
    )
    total_rows = owners * capacity
    block_rows = math.gcd(total_rows, 1024)
    table = onehot_sum(
        got_slots.reshape(total_rows), got_rows.reshape(total_rows, width), OWN_ROWS, block_rows
    )
    return table.reshape(1, OWN_ROWS, width)


def per_device(hot_ids, hot_grads, cold_grads, cold_slots, cold_counts):
    hot_grad = hot_part(hot_ids, hot_grads)
    cold_grad = cold_part(cold_grads, cold_slots, cold_counts)
    return (hot_grad, cold_grad)


def solution(mesh):
    return jax.shard_map(
        per_device,
        mesh=mesh,
        in_specs=(
            P(("gx", "gy")),
            P(("gx", "gy"), None),
            P("gx", "gy", None, None, None),
            P("gx", "gy", None, None),
            P("gx", "gy", None),
        ),
        out_specs=(P(), P("gx", "gy", None)),
        check_vma=False,
    )
```

profile of v0, /device:TPU:0, one launch (start us, length us, event | category | flops | bytes accessed | tf_op | source)
XLA Modules:
  0.0 185.8 jit_solution(4274179711939193013)
XLA Ops:
  7.2 0.0 reduce-scatter.2.cloned.1.call-start
  7.2 0.8 reshape.43
  8.0 0.0 copy-start.2
  8.0 0.0 copy-start.3
  8.0 0.0 copy-start
  8.0 17.7 %while.22 = (s32[]{:T(128)}, f32[2048,128]{1,0:T(8,128)S(1)}, s32[4,2048]{1,0:T(4,128)S(1)}, bf16[4,2048,128]{2,1,0:T(8,128)(2,1)}, s32[]{:T(128)}, /*index=5*/s32[]{:T(128)}) while((s32[]{:T(128)}, f32[2048,128]{1,0:T(8,128)S(1)}, s32[4,2048]{1,0:T(4,128)S(1)}, bf16[4,2048,128]{2,1,0:T(8,128)(2,1)}, s32[]{:T(128)}, ...), condition=%wide.region_1.2_spmd.clone, body=%wide.region_0.1_spmd.clone.sunk | while | flops 1078460416 | bytes 2646611 | solution.py:24
  8.1 4.4 %fusion.21 = f32[2048,128]{1,0:T(8,128)S(1)} fusion(s32[2048]{0:T(1024)S(1)} %bitcast.25, f32[2048,128]{1,0:T(8,128)S(1)} %get-tuple-element.165, bf16[4,2048,128]{2,1,0:T(8,128)(2,1)} %get-tuple-element.173, s32[]{:T(128)} %get-tuple-element.164, pred[]{:T(512)S(6)} %compare.6), kind=kOutput, calls=%fused_computation.5.clone.1 | convolution fusion | flops 1078460416 | bytes 2630145 | tf_op jit(solution)/shard_map/while/body/eval_jaxpr/dot_general | solution.py:21
  12.6 4.4 %fusion.21 = f32[2048,128]{1,0:T(8,128)S(1)} fusion(s32[2048]{0:T(1024)S(1)} %bitcast.25, f32[2048,128]{1,0:T(8,128)S(1)} %get-tuple-element.165, bf16[4,2048,128]{2,1,0:T(8,128)(2,1)} %get-tuple-element.173, s32[]{:T(128)} %get-tuple-element.164, pred[]{:T(512)S(6)} %compare.6), kind=kOutput, calls=%fused_computation.5.clone.1 | convolution fusion | flops 1078460416 | bytes 2630145 | tf_op jit(solution)/shard_map/while/body/eval_jaxpr/dot_general | solution.py:21
  17.0 4.4 %fusion.21 = f32[2048,128]{1,0:T(8,128)S(1)} fusion(s32[2048]{0:T(1024)S(1)} %bitcast.25, f32[2048,128]{1,0:T(8,128)S(1)} %get-tuple-element.165, bf16[4,2048,128]{2,1,0:T(8,128)(2,1)} %get-tuple-element.173, s32[]{:T(128)} %get-tuple-element.164, pred[]{:T(512)S(6)} %compare.6), kind=kOutput, calls=%fused_computation.5.clone.1 | convolution fusion | flops 1078460416 | bytes 2630145 | tf_op jit(solution)/shard_map/while/body/eval_jaxpr/dot_general | solution.py:21
  21.4 4.4 %fusion.21 = f32[2048,128]{1,0:T(8,128)S(1)} fusion(s32[2048]{0:T(1024)S(1)} %bitcast.25, f32[2048,128]{1,0:T(8,128)S(1)} %get-tuple-element.165, bf16[4,2048,128]{2,1,0:T(8,128)(2,1)} %get-tuple-element.173, s32[]{:T(128)} %get-tuple-element.164, pred[]{:T(512)S(6)} %compare.6), kind=kOutput, calls=%fused_computation.5.clone.1 | convolution fusion | flops 1078460416 | bytes 2630145 | tf_op jit(solution)/shard_map/while/body/eval_jaxpr/dot_general | solution.py:21
  25.7 0.0 copy-start.1
  25.8 1.0 copy-done.1
  26.7 0.0 reduce-scatter.2.cloned.1.call-update
  26.7 0.0 copy-done.2
  26.8 0.6 all_to_all.9
  27.4 7.3 %all-to-all-start = ((s32[8,1,512]{2,1,0:T(1,128)}), s32[8,1,512]{2,1,0:T(1,128)S(1)}, u32[]{:S(2)}, u32[]{:S(2)}) async-start(s32[8,1,512]{2,1,0:T(1,128)} %all_to_all.9), calls=%async_computation.1 | async-start | bytes 32768 | tf_op jit(solution)/shard_map/all_to_all | solution.py:49
  34.7 0.0 copy-done.3
  34.7 0.1 iota_compare_fusion.8
  34.8 0.0 copy-done
  34.8 1.5 bitcast_select_fusion
  36.2 5.1 %all-to-all-done = s32[8,1,512]{2,1,0:T(1,128)S(1)} async-done(((s32[8,1,512]{2,1,0:T(1,128)}), s32[8,1,512]{2,1,0:T(1,128)S(1)}, u32[]{:S(2)}, u32[]{:S(2)}) %all-to-all-start) | async-done | bytes 16416 | tf_op jit(solution)/shard_map/all_to_all | solution.py:49
  41.3 3.6 %all-to-all-start.1 = ((bf16[8,512,128]{2,1,0:T(8,128)(2,1)}), bf16[8,512,128]{2,1,0:T(8,128)(2,1)S(1)}, u32[]{:S(2)}, u32[]{:S(2)}) async-start(bf16[8,512,128]{2,1,0:T(8,128)(2,1)} %bitcast_select_fusion), calls=%async_computation.2 | async-start | bytes 2097152 | tf_op jit(solution)/shard_map/all_to_all | solution.py:48
  44.9 0.0 all-reduce.2.cloned.1.call-start
  44.9 56.6 %reduce-scatter.2.cloned.1.call-done = f32[256,128]{1,0:T(8,128)} async-done(((f32[2048,128]{1,0:T(8,128)}), f32[256,128]{1,0:T(8,128)}) %reduce-scatter.2.cloned.1.call-update) | async-done | bytes 131088 | tf_op jit(solution)/shard_map/reduce_scatter | solution.py:33
  101.6 0.0 all-reduce.2.cloned.1.call-update
  101.6 0.0 all-gather.2.cloned.1.call-start
  101.6 32.9 %all-reduce.2.cloned.1.call-done = f32[256,128]{1,0:T(8,128)} async-done(((f32[256,128]{1,0:T(8,128)}), f32[256,128]{1,0:T(8,128)}) %all-reduce.2.cloned.1.call-update) | async-done | bytes 131088 | tf_op jit(solution)/shard_map/psum | solution.py:34
  134.6 0.0 all-gather.2.cloned.1.call-update
  134.7 0.0 all-to-all-done.1
  134.7 7.3 %while.23 = (s32[]{:T(128)}, f32[2048,128]{1,0:T(8,128)S(1)}, s32[4,1024]{1,0:T(4,128)S(1)}, bf16[4,1024,128]{2,1,0:T(8,128)(2,1)S(1)}, s32[]{:T(128)}, /*index=5*/s32[]{:T(128)}) while((s32[]{:T(128)}, f32[2048,128]{1,0:T(8,128)S(1)}, s32[4,1024]{1,0:T(4,128)S(1)}, bf16[4,1024,128]{2,1,0:T(8,128)(2,1)S(1)}, s32[]{:T(128)}, ...), condition=%wide.region_5.6_spmd.clone, body=%wide.region_4.5_spmd.clone.sunk | while | flops 539492352 | bytes 2371671 | solution.py:24
  134.7 1.8 fusion.23
  136.5 1.8 fusion.23
  138.4 1.8 fusion.23
  140.2 1.8 fusion.23
  142.0 0.0 copy-start.4
  142.0 35.0 %all-gather.2.cloned.1.call-done = f32[2048,128]{1,0:T(8,128)} async-done(((f32[256,128]{1,0:T(8,128)}), f32[2048,128]{1,0:T(8,128)}) %all-gather.2.cloned.1.call-update) | async-done | bytes 1048592 | tf_op jit(solution)/shard_map/all_gather | solution.py:35
  177.0 2.3 %broadcast_multiply_fusion = f32[2048,128]{1,0:T(8,128)} fusion(f32[2048,128]{1,0:T(8,128)} %all-gather.2.cloned.1.call-done), kind=kLoop, calls=%fused_computation.19 | loop fusion | flops 262144 | bytes 2097152 | tf_op jit(solution)/shard_map/mul | solution.py:36
  179.3 0.0 copy-done.4
  (12 shorter events, 0.1 us)
Async XLA Ops:
  7.2 94.4 %reduce-scatter.2.cloned.1.call-start = ((), (), s32[]{:S(2)}) async-start(), calls=%async_computation.3 | async-start | bytes 1179648 | tf_op jit(solution)/shard_map/reduce_scatter | solution.py:33
  8.0 18.8 %copy-start.2 = (s32[1,1,8,512]{3,2,1,0:T(8,128)S(1)}, s32[1,1,8,512]{3,2,1,0:T(8,128)}, u32[]{:S(2)}) copy-start(s32[1,1,8,512]{3,2,1,0:T(8,128)} %param.12) | copy-start | bytes 49156
  8.0 26.7 %copy-start.3 = (s32[1,1,8]{2,1,0:T(1,128)S(1)}, s32[1,1,8]{2,1,0:T(1,128)}, u32[]{:S(2)}) copy-start(s32[1,1,8]{2,1,0:T(1,128)} %param.13) | copy-start | bytes 100
  8.0 26.7 %copy-start = (bf16[1,1,8,512,128]{4,3,2,1,0:T(8,128)(2,1)S(1)}, bf16[1,1,8,512,128]{4,3,2,1,0:T(8,128)(2,1)}, u32[]{:S(2)}) copy-start(bf16[1,1,8,512,128]{4,3,2,1,0:T(8,128)(2,1)} %param.11) | copy-start | bytes 3145732
  25.7 1.0 copy-start.1
  27.4 13.9 %all-to-all-start = ((s32[8,1,512]{2,1,0:T(1,128)}), s32[8,1,512]{2,1,0:T(1,128)S(1)}, u32[]{:S(2)}, u32[]{:S(2)}) async-start(s32[8,1,512]{2,1,0:T(1,128)} %all_to_all.9), calls=%async_computation.1 | async-start | bytes 32768 | tf_op jit(solution)/shard_map/all_to_all | solution.py:49
  41.3 93.4 %all-to-all-start.1 = ((bf16[8,512,128]{2,1,0:T(8,128)(2,1)}), bf16[8,512,128]{2,1,0:T(8,128)(2,1)S(1)}, u32[]{:S(2)}, u32[]{:S(2)}) async-start(bf16[8,512,128]{2,1,0:T(8,128)(2,1)} %bitcast_select_fusion), calls=%async_computation.2 | async-start | bytes 2097152 | tf_op jit(solution)/shard_map/all_to_all | solution.py:48
  44.9 89.7 %all-reduce.2.cloned.1.call-start = ((), (), s32[]{:S(2)}) async-start(), calls=%async_computation.4 | async-start | bytes 262144 | tf_op jit(solution)/shard_map/psum | solution.py:34
  101.6 75.4 %all-gather.2.cloned.1.call-start = ((), (), s32[]{:S(2)}) async-start(), calls=%async_computation.5 | async-start | bytes 1179648 | tf_op jit(solution)/shard_map/all_gather | solution.py:35
  142.0 37.3 %copy-start.4 = (f32[2048,128]{1,0:T(8,128)}, f32[2048,128]{1,0:T(8,128)S(1)}, u32[]{:S(2)}) copy-start(f32[2048,128]{1,0:T(8,128)S(1)} %get-tuple-element.57) | copy-start | bytes 3145732
Sparse Core Ops, SparseCore 0:
  26.9 74.6 reduce-scatter.1
  103.9 30.6 all-reduce.1
  136.7 40.2 all-gather.1
where the time goes:
time: 186 us
  waiting for transfers between devices  130 us (70%)
  matrix products  24.7 us (13%)
  between operations  13.9 us (7%)
  starting transfers between devices  11 us (6%)
  other arithmetic  3.89 us (2%)
  local copies, waits for them, and re-layouts  2.47 us (1%)
    reduce_scatter x1, waiting for transfers between devices, hot_part(): shared = lax.psum_scatter(local_sum, 'gy', scatter_dimension=0, tiled=True)  56.6 us
    all_gather x1, waiting for transfers between devices, hot_part(): total = lax.all_gather(shared, 'gy', axis=0, tiled=True)  35 us
    psum x1, waiting for transfers between devices, hot_part(): shared = lax.psum(shared, 'gx')  32.9 us
    dot_general x8, matrix products, add_block(): jnp.dot(selector, data_here, preferred_element_type=jnp.float32)  24.7 us
    all_to_all x1, starting transfers between devices, cold_part(): lax.all_to_all(slots_here, 'gy', split_axis=0, concat_axis=0, tiled=True)  7.31 us
    all_to_all x1, waiting for transfers between devices, cold_part(): lax.all_to_all(slots_here, 'gy', split_axis=0, concat_axis=0, tiled=True)  5.07 us
  transfers between devices with their start and end apart: 5, of which 4 were waited for; matrix products, arithmetic and copies ran while one was open for 5% of the time, Pallas kernels for 0%

commit v1 on v0

v1 whole, which is shorter than its diff:
```python
import functools

import jax
import jax.numpy as jnp
from jax import lax
from jax.experimental import pallas as pl
from jax.experimental.pallas import tpu as pltpu
from jax.sharding import PartitionSpec as P

HOT = 2048
OWN_ROWS = 2048
LANES = 128
HIGH = 4
MESH = pl.DeviceIdType.MESH


def add_block(acc, ids, data, pieces, low_rows):
    columns = ids.T
    lo_iota = lax.broadcasted_iota(jnp.int32, (low_rows, LANES), 0)
    selectors, rows = [], []
    for j in range(pieces):
        lo = jnp.bitwise_and(ids[j : j + 1, :], low_rows - 1)
        selectors.append(jnp.where(lo_iota == lo, 1.0, 0.0).astype(jnp.bfloat16))
        here = data[j * LANES : (j + 1) * LANES, :]
        column = jnp.broadcast_to(columns[:, j : j + 1], here.shape)
        parts = []
        for h in range(HIGH):
            inside = (column >= h * low_rows) & (column < (h + 1) * low_rows)
            parts.append(here * jnp.where(inside, 1.0, 0.0).astype(jnp.bfloat16))
        rows.append(jnp.concatenate(parts, axis=1))
    selector = jnp.concatenate(selectors, axis=1)
    spread = jnp.concatenate(rows, axis=0)
    acc[...] += jnp.dot(selector, spread, preferred_element_type=jnp.float32)


def kernel(
    nx, ny, factor, cap_pieces,
    ids_ref, hot_ref, slots_ref, cold_ref, hot_out, cold_out,
    acc, cacc, tab, full, crecv, srecv, r0, r1, r2, r3,
    csend, crsem, ssend, srsem, own_sem, hsend, hrecv,
):
    gx, gy = lax.axis_index("gx"), lax.axis_index("gy")
    px, py = 2 - nx % 2, 2 - ny % 2
    low_rows = HOT // HIGH
    own_low = OWN_ROWS // HIGH
    width = hot_ref.shape[1]

    stages = [
        (px, lax.rem(gx, px), lambda p: ((gx // px) * px + p, gy)),
        (nx // px, gx // px, lambda p: (p * px + lax.rem(gx, px), gy)),
        (py, lax.rem(gy, py), lambda p: (gx, (gy // py) * py + p)),
        (ny // py, gy // py, lambda p: (gx, p * py + lax.rem(gy, py))),
    ]
    barrier = pltpu.get_barrier_semaphore()
    greeted = 0
    for n, k, device in stages[:2]:
        for j in range(1, n):
            pl.semaphore_signal(barrier, inc=1, device_id=device(lax.rem(k + j, n)), device_id_type=MESH)
            greeted += 1
    for j in range(1, ny):
        pl.semaphore_signal(barrier, inc=1, device_id=(gx, lax.rem(gy + j, ny)), device_id_type=MESH)
        greeted += 1
    pl.semaphore_wait(barrier, greeted)

    def cold_copies(j):
        peer = lax.rem(gy + j, ny)
        return (
            pltpu.make_async_remote_copy(
                src_ref=cold_ref.at[peer], dst_ref=crecv.at[j],
                send_sem=csend.at[j], recv_sem=crsem.at[j],
                device_id=(gx, peer), device_id_type=MESH,
            ),
            pltpu.make_async_remote_copy(
                src_ref=slots_ref.at[peer], dst_ref=srecv.at[j],
                send_sem=ssend.at[j], recv_sem=srsem.at[j],
                device_id=(gx, peer), device_id_type=MESH,
            ),
        )

    for j in range(1, ny):
        for copy in cold_copies(j):
            copy.start()
    own = pltpu.make_async_copy(cold_ref.at[gy], crecv.at[0], own_sem)
    own.start()

    acc[...] = jnp.zeros_like(acc)
    cacc[...] = jnp.zeros_like(cacc)

    def hot_step(i, carry):
        pieces = ids_ref.shape[1]
        data = hot_ref[pl.ds(pl.multiple_of(i * pieces * LANES, LANES), pieces * LANES), :]
        add_block(acc, ids_ref[i], data, pieces, low_rows)
        return carry

    lax.fori_loop(0, ids_ref.shape[0], hot_step, 0)
    for h in range(HIGH):
        tab[h * low_rows : (h + 1) * low_rows, :] = acc[:, h * width : (h + 1) * width]

    base, size = 0, HOT
    used = 0
    regions = []
    for (n, k, device), landing in zip(stages, (r0, r1, r2, r3)):
        regions.append((base, size))
        sub = size // n
        copies = []
        for j in range(1, n):
            peer = lax.rem(k + j, n)
            copies.append(
                pltpu.make_async_remote_copy(
                    src_ref=tab.at[pl.ds(pl.multiple_of(base + peer * sub, 8), sub), :],
                    dst_ref=landing.at[j - 1],
                    send_sem=hsend.at[used], recv_sem=hrecv.at[used],
                    device_id=device(peer), device_id_type=MESH,
                )
            )
            used += 1
        for copy in copies:
            copy.start()
        for copy in copies:
            copy.wait()
        base, size = base + k * sub, sub
        if n > 1:
            rows = pl.ds(pl.multiple_of(base, 8), size)
            total = tab[rows, :]
            for j in range(1, n):
                total = total + landing[j - 1]
            tab[rows, :] = total

    rows = pl.ds(pl.multiple_of(base, 8), size)
    full[rows, :] = tab[rows, :] * factor

    def cold_all():
        own.wait()
        add_block(cacc, slots_ref[gy], crecv[0], cap_pieces, own_low)

        def cold_step(j, carry):
            for copy in cold_copies(j):
                copy.wait()
            add_block(cacc, srecv[j], crecv[j], cap_pieces, own_low)
            return carry

        lax.fori_loop(1, ny, cold_step, 0)
        for h in range(HIGH):
            cold_out[h * own_low : (h + 1) * own_low, :] = cacc[:, h * width : (h + 1) * width]

    for index in (3, 2, 1, 0):
        n, k, device = stages[index]
        copies = []
        for j in range(1, n):
            rows = pl.ds(pl.multiple_of(base, 8), size)
            copies.append(
                pltpu.make_async_remote_copy(
                    src_ref=full.at[rows, :], dst_ref=full.at[rows, :],
                    send_sem=hsend.at[used], recv_sem=hrecv.at[used],
                    device_id=device(lax.rem(k + j, n)), device_id_type=MESH,
                )
            )
            used += 1
        for copy in copies:
            copy.start()
        if index == 1:
            cold_all()
        for j, copy in enumerate(copies, 1):
            copy.wait_send()
            source = regions[index][0] + lax.rem(k - j + n, n) * size
            rows = pl.ds(pl.multiple_of(source, 8), size)
            pltpu.make_async_remote_copy(
                src_ref=full.at[rows, :], dst_ref=full.at[rows, :],
                send_sem=hsend.at[used - n + j], recv_sem=hrecv.at[used - n + j],
                device_id=device(lax.rem(k + j, n)), device_id_type=MESH,
            ).wait_recv()
        base, size = regions[index]
    hot_out[...] = full[...]


def per_device(nx, ny, hot_ids, hot_grads, cold_grads, cold_slots, cold_counts):
    look, width = hot_grads.shape
    owners, capacity = cold_slots.shape[2], cold_slots.shape[3]
    px, py = 2 - nx % 2, 2 - ny % 2
    factor = (HOT / (look * nx * ny)) ** 0.5
    places = lax.broadcasted_iota(jnp.int32, (owners, capacity), 1)
    slots = jnp.where(places < cold_counts.reshape(owners, 1), cold_slots.reshape(owners, capacity), -1)
    cap_pieces = capacity // LANES
    slots = slots.reshape(owners, cap_pieces, LANES)
    pad = -cap_pieces % 8
    slots = jnp.pad(slots, ((0, 0), (0, pad), (0, 0)), constant_values=-1)
    ids = hot_ids.reshape(-1, 8, LANES)
    s0 = HOT // px
    s1 = s0 // (nx // px)
    s2 = s1 // py
    s3 = s2 // (ny // py)
    n_hot = 2 * ((px - 1) + (nx // px - 1) + (py - 1) + (ny // py - 1))
    f32 = jnp.float32
    vmem = pl.BlockSpec(memory_space=pltpu.VMEM)
    hot, cold = pl.pallas_call(
        functools.partial(kernel, nx, ny, factor, cap_pieces),
        out_shape=(
            jax.ShapeDtypeStruct((HOT, width), f32),
            jax.ShapeDtypeStruct((OWN_ROWS, width), f32),
        ),
        in_specs=[vmem, vmem, vmem, pl.BlockSpec(memory_space=pl.ANY)],
        out_specs=(vmem, vmem),
        scratch_shapes=[
            pltpu.VMEM((HOT // HIGH, HIGH * width), f32),
            pltpu.VMEM((OWN_ROWS // HIGH, HIGH * width), f32),
            pltpu.VMEM((HOT, width), f32),
            pltpu.VMEM((HOT, width), f32),
            pltpu.VMEM((owners, capacity, width), jnp.bfloat16),
            pltpu.VMEM((owners, cap_pieces + pad, LANES), jnp.int32),
            pltpu.VMEM((max(px - 1, 1), s0, width), f32),
            pltpu.VMEM((max(nx // px - 1, 1), s1, width), f32),
            pltpu.VMEM((max(py - 1, 1), s2, width), f32),
            pltpu.VMEM((max(ny // py - 1, 1), s3, width), f32),
            pltpu.SemaphoreType.DMA((owners,)),
            pltpu.SemaphoreType.DMA((owners,)),
            pltpu.SemaphoreType.DMA((owners,)),
            pltpu.SemaphoreType.DMA((owners,)),
            pltpu.SemaphoreType.DMA,
            pltpu.SemaphoreType.DMA((n_hot,)),
            pltpu.SemaphoreType.DMA((n_hot,)),
        ],
        compiler_params=pltpu.CompilerParams(
            collective_id=0, has_side_effects=True, vmem_limit_bytes=32 * 1024 * 1024
        ),
    )(ids, hot_grads, slots, cold_grads.reshape(owners, capacity, width))
    return hot, cold.reshape(1, OWN_ROWS, width)


def solution(mesh):
    body = functools.partial(per_device, mesh.shape["gx"], mesh.shape["gy"])
    return jax.shard_map(
        body,
        mesh=mesh,
        in_specs=(
            P(("gx", "gy")),
            P(("gx", "gy"), None),
            P("gx", "gy", None, None, None),
            P("gx", "gy", None, None),
            P("gx", "gy", None),
        ),
        out_specs=(P(), P("gx", "gy", None)),
        check_vma=False,
    )
```

time: 186 us -> 59.9 us (0.32)
  waiting for transfers between devices: 130 us -> 0 us
  Pallas kernels: 0 us -> 52 us
  matrix products: 24.7 us -> 0 us
  between operations: 13.9 us -> 0.66 us
  starting transfers between devices: 11 us -> 0 us
  local copies, waits for them, and re-layouts: 2.47 us -> 6.25 us
  other arithmetic: 3.89 us -> 0.73 us
    reduce_scatter x1 -> x0, waiting for transfers between devices: 56.6 us -> none  [hot_part(): shared = lax.psum_scatter(local_sum, 'gy', scatter_dimension=0, tiled=True)]
    pallas_call x0 -> x1, Pallas kernels: none -> 52 us  [per_device(): pl.pallas_call(functools.partial(kernel, nx, ny, factor, cap_pieces), out...]
    all_gather x1 -> x0, waiting for transfers between devices: 35 us -> none  [hot_part(): total = lax.all_gather(shared, 'gy', axis=0, tiled=True)]
    psum x1 -> x0, waiting for transfers between devices: 32.9 us -> none  [hot_part(): shared = lax.psum(shared, 'gx')]
    dot_general x8 -> x0, matrix products: 24.7 us -> none  [add_block(): jnp.dot(selector, data_here, preferred_element_type=jnp.float32)]
    all_to_all x2 -> x0, starting transfers between devices: 10.9 us -> none  [the longest x1 7.31 us: cold_part(): lax.all_to_all(slots_here, 'gy', split_axis=0, concat_axis=0, tiled=True)]
    all_to_all x2 -> x0, waiting for transfers between devices: 5.07 us -> none  [the longest x1 5.07 us: cold_part(): lax.all_to_all(slots_here, 'gy', split_axis=0, concat_axis=0, tiled=True)]
    unnamed x10 -> x8, local copies, waits for them, and re-layouts: 0.99 us -> 5.51 us
  transfers between devices with their start and end apart: 5 -> 0, of which waited for: 4 -> 0; matrix products, arithmetic and copies ran while one was open for 5% -> 0% of each run, Pallas kernels for 0% -> 0%
where the time goes in v1:
time: 59.9 us; the launch traced here: 59.6 us
  Pallas kernels  52 us (87%)
  local copies, waits for them, and re-layouts  6.25 us (10%)
  other arithmetic  0.73 us (1%)
  between operations  0.66 us (1%)
    pallas_call x1, Pallas kernels, per_device(): pl.pallas_call(functools.partial(kernel, nx, ny, factor, cap_pieces), out...  52 us
    unnamed x8, local copies, waits for them, and re-layouts  5.51 us

profile of v1, /device:TPU:0, one launch (start us, length us, event | category | flops | bytes accessed | tf_op | source)
XLA Modules:
  0.0 59.6 jit_solution(10383326531417773386)
XLA Ops:
  0.6 0.7 %reshape.35 = s32[8,4,128]{2,1,0:T(4,128)S(1)} reshape(s32[1,1,8,512]{3,2,1,0:T(8,128)} %param.8) | data formatting | bytes 32768 | tf_op jit(solution)/shard_map/reshape | solution.py:182
  1.4 0.7 %compare_select_fusion = s32[8,4,128]{2,1,0:T(4,128)S(1)} fusion(s32[8,4,128]{2,1,0:T(4,128)S(1)} %reshape.35, s32[4,128]{1,0:T(4,128)S(1)} %multiply_add_fusion, s32[8]{0:T(128)} %bitcast.9), kind=kLoop, calls=%fused_computation | loop fusion | flops 8192 | bytes 34848 | tf_op jit(solution)/shard_map/jit(_where)/select_n | solution.py:182
  2.1 0.0 copy-start
  2.1 1.6 %copy-done = bf16[8192,128]{1,0:T(8,128)(2,1)S(1)} copy-done((bf16[8192,128]{1,0:T(8,128)(2,1)S(1)}, bf16[8192,128]{1,0:T(8,128)(2,1)}, u32[]{:S(2)}) %copy-start) | copy-done | bytes 2097176
  3.7 0.0 copy-start.1
  3.7 1.2 %copy-done.1 = bf16[1,1,8,512,128]{4,3,2,1,0:T(8,128)(2,1)S(1)} copy-done((bf16[1,1,8,512,128]{4,3,2,1,0:T(8,128)(2,1)S(1)}, bf16[1,1,8,512,128]{4,3,2,1,0:T(8,128)(2,1)}, u32[]{:S(2)}) %copy-start.1) | copy-done | bytes 1048600
  4.9 0.0 copy-start.2
  4.9 0.8 %copy-done.2 = s32[8192]{0:T(1024)S(1)} copy-done((s32[8192]{0:T(1024)S(1)}, s32[8192]{0:T(1024)}, u32[]{:S(2)}) %copy-start.2) | copy-done | bytes 32792
  5.7 52.0 %shard_map.68 = (f32[2048,128]{1,0:T(8,128)S(1)}, f32[2048,128]{1,0:T(8,128)S(1)}) custom-call(s32[8,8,128]{2,1,0:T(8,128)S(1)} %bitcast.8, bf16[8192,128]{1,0:T(8,128)(2,1)S(1)} %copy-done, s32[8,8,128]{2,1,0:T(8,128)S(1)} %pad.4.slots_ref, bf16[8,512,128]{2,1,0:T(8,128)(2,1)S(1)} %bitcast.6), custom_call_target="tpu_custom_call" | custom-call | tf_op jit(solution)/shard_map/pallas_call | solution.py:195
  57.7 1.0 %copy.9 = f32[2048,128]{1,0:T(8,128)} copy(f32[2048,128]{1,0:T(8,128)S(1)} %get-tuple-element.8) | data formatting | bytes 2097152
  58.7 1.0 %copy.10 = f32[1,2048,128]{2,1,0:T(8,128)} copy(f32[1,2048,128]{2,1,0:T(8,128)S(1)} %bitcast.7) | data formatting | bytes 2097152
  (2 shorter events, 0.0 us)
Async XLA Ops:
  2.1 1.6 %copy-start = (bf16[8192,128]{1,0:T(8,128)(2,1)S(1)}, bf16[8192,128]{1,0:T(8,128)(2,1)}, u32[]{:S(2)}) copy-start(bf16[8192,128]{1,0:T(8,128)(2,1)} %hot_ref.1) | copy-start | bytes 6291460
  3.7 1.2 %copy-start.1 = (bf16[1,1,8,512,128]{4,3,2,1,0:T(8,128)(2,1)S(1)}, bf16[1,1,8,512,128]{4,3,2,1,0:T(8,128)(2,1)}, u32[]{:S(2)}) copy-start(bf16[1,1,8,512,128]{4,3,2,1,0:T(8,128)(2,1)} %param.7) | copy-start | bytes 3145732
  4.9 0.8 %copy-start.2 = (s32[8192]{0:T(1024)S(1)}, s32[8192]{0:T(1024)}, u32[]{:S(2)}) copy-start(s32[8192]{0:T(1024)} %param.5) | copy-start | bytes 98308

commit v2 on v1

v2 whole, which is shorter than its diff:
```python
import functools

import jax
import jax.numpy as jnp
from jax import lax
from jax.experimental import pallas as pl
from jax.experimental.pallas import tpu as pltpu
from jax.sharding import PartitionSpec as P

HOT = 2048
OWN_ROWS = 2048
LANES = 128
HIGH = 4
MESH = pl.DeviceIdType.MESH


def add_block(acc, ids, data, pieces, low_rows):
    columns = ids.T
    lo_iota = lax.broadcasted_iota(jnp.int32, (low_rows, LANES), 0)
    selectors, rows = [], []
    for j in range(pieces):
        lo = jnp.bitwise_and(ids[j : j + 1, :], low_rows - 1)
        selectors.append(jnp.where(lo_iota == lo, 1.0, 0.0).astype(jnp.bfloat16))
        here = data[j * LANES : (j + 1) * LANES, :]
        column = jnp.broadcast_to(columns[:, j : j + 1], here.shape)
        parts = []
        for h in range(HIGH):
            inside = (column >= h * low_rows) & (column < (h + 1) * low_rows)
            parts.append(here * jnp.where(inside, 1.0, 0.0).astype(jnp.bfloat16))
        rows.append(jnp.concatenate(parts, axis=1))
    selector = jnp.concatenate(selectors, axis=1)
    spread = jnp.concatenate(rows, axis=0)
    acc[...] += jnp.dot(selector, spread, preferred_element_type=jnp.float32)


def kernel(
    nx, ny, factor, cap_pieces,
    ids_ref, hot_ref, slots_ref, cold_ref, hot_out, cold_out,
    acc, cacc, tab, full, hotv, idsv, crecv, srecv, r0, a1, b1, a2, b2, a3, b3,
    csend, crsem, ssend, srsem, own_sem, hsend, hrecv,
):
    gx, gy = lax.axis_index("gx"), lax.axis_index("gy")
    px, py = 2 - nx % 2, 2 - ny % 2
    low_rows = HOT // HIGH
    own_low = OWN_ROWS // HIGH
    width = hot_ref.shape[1]
    landing_refs = (a1, b1, a2, b2, a3, b3)

    core = (px, lax.rem(gx, px), lambda p: ((gx // px) * px + p, gy))
    along_x = (nx // px, gx // px, lambda p: (p * px + lax.rem(gx, px), gy))
    pair_y = (py, lax.rem(gy, py), lambda p: (gx, (gy // py) * py + p))
    rest_y = (ny // py, gy // py, lambda p: (gx, p * py + lax.rem(gy, py)))
    chains = [[along_x, pair_y, rest_y], [pair_y, along_x, rest_y]]

    hot_copy = pltpu.make_async_copy(hot_ref, hotv, own_sem.at[1])
    ids_copy = pltpu.make_async_copy(ids_ref, idsv, own_sem.at[2])
    own = pltpu.make_async_copy(cold_ref.at[gy], crecv.at[0], own_sem.at[0])
    ids_copy.start()
    hot_copy.start()

    barrier = pltpu.get_barrier_semaphore()
    greeted = 0
    for n, k, device in (core, along_x):
        for j in range(1, n):
            pl.semaphore_signal(barrier, inc=1, device_id=device(lax.rem(k + j, n)), device_id_type=MESH)
            greeted += 1
    for j in range(1, ny):
        pl.semaphore_signal(barrier, inc=1, device_id=(gx, lax.rem(gy + j, ny)), device_id_type=MESH)
        greeted += 1
    pl.semaphore_wait(barrier, greeted)

    def cold_copies(j):
        peer = lax.rem(gy + j, ny)
        return (
            pltpu.make_async_remote_copy(
                src_ref=cold_ref.at[peer], dst_ref=crecv.at[j],
                send_sem=csend.at[j], recv_sem=crsem.at[j],
                device_id=(gx, peer), device_id_type=MESH,
            ),
            pltpu.make_async_remote_copy(
                src_ref=slots_ref.at[peer], dst_ref=srecv.at[j],
                send_sem=ssend.at[j], recv_sem=srsem.at[j],
                device_id=(gx, peer), device_id_type=MESH,
            ),
        )

    middle = ny // 2
    for j in range(1, ny):
        if j != middle:
            for copy in cold_copies(j):
                copy.start()
    own.start()

    acc[...] = jnp.zeros_like(acc)
    cacc[...] = jnp.zeros_like(cacc)
    ids_copy.wait()
    hot_copy.wait()

    def hot_step(i, carry):
        pieces = idsv.shape[1]
        data = hotv[pl.ds(pl.multiple_of(i * pieces * LANES, LANES), pieces * LANES), :]
        add_block(acc, idsv[i], data, pieces, low_rows)
        return carry

    lax.fori_loop(0, idsv.shape[0], hot_step, 0)
    for h in range(HIGH):
        tab[h * low_rows : (h + 1) * low_rows, :] = acc[:, h * width : (h + 1) * width]

    used = 0

    def scatter_start(stage, base, size, landing):
        nonlocal used
        n, k, device = stage
        sub = size // n
        copies = []
        for j in range(1, n):
            peer = lax.rem(k + j, n)
            copies.append(
                pltpu.make_async_remote_copy(
                    src_ref=tab.at[pl.ds(pl.multiple_of(base + peer * sub, 8), sub), :],
                    dst_ref=landing.at[j - 1],
                    send_sem=hsend.at[used], recv_sem=hrecv.at[used],
                    device_id=device(peer), device_id_type=MESH,
                )
            )
            copies[-1].start()
            used += 1
        return copies

    def scatter_end(copies, stage, base, size, landing):
        n, k, device = stage
        for copy in copies:
            copy.wait()
        sub = size // n
        base = base + k * sub
        if n > 1:
            rows = pl.ds(pl.multiple_of(base, 8), sub)
            total = tab[rows, :]
            for j in range(1, n):
                total = total + landing[j - 1]
            tab[rows, :] = total
        return base, sub

    def gather_start(stage, base, size):
        nonlocal used
        n, k, device = stage
        rows = pl.ds(pl.multiple_of(base, 8), size)
        first = used
        for j in range(1, n):
            pltpu.make_async_remote_copy(
                src_ref=full.at[rows, :], dst_ref=full.at[rows, :],
                send_sem=hsend.at[used], recv_sem=hrecv.at[used],
                device_id=device(lax.rem(k + j, n)), device_id_type=MESH,
            ).start()
            used += 1
        return first

    def gather_end(first, stage, base, size):
        n, k, device = stage
        for j in range(1, n):
            mine = pl.ds(pl.multiple_of(base, 8), size)
            theirs = pl.ds(pl.multiple_of(base + (lax.rem(k - j + n, n) - k) * size, 8), size)
            for rows, receive in ((mine, False), (theirs, True)):
                copy = pltpu.make_async_remote_copy(
                    src_ref=full.at[rows, :], dst_ref=full.at[rows, :],
                    send_sem=hsend.at[first + j - 1], recv_sem=hrecv.at[first + j - 1],
                    device_id=device(lax.rem(k + j, n)), device_id_type=MESH,
                )
                if receive:
                    copy.wait_recv()
                else:
                    copy.wait_send()

    def cold_range(start, stop):
        def cold_step(j, carry):
            for copy in cold_copies(j):
                copy.wait()
            add_block(cacc, srecv[j], crecv[j], cap_pieces, own_low)
            return carry

        lax.fori_loop(start, stop, cold_step, 0)

    copies = scatter_start(core, 0, HOT, r0)
    own.wait()
    add_block(cacc, slots_ref[gy], crecv[0], cap_pieces, own_low)
    base, size = scatter_end(copies, core, 0, HOT, r0)
    top = (base, size)
    half = size // 2
    places = [(base, half), (base + half, half)]
    history = []
    for step in range(3):
        landings = [landing_refs[2 * step], landing_refs[2 * step + 1]]
        history.append(list(places))
        pending = [
            scatter_start(chains[c][step], *places[c], landings[c]) for c in range(2)
        ]
        if step == 1:
            cold_range(1, middle // 2 + 1)
        if step == 2:
            cold_range(middle // 2 + 1, middle)
        places = [
            scatter_end(pending[c], chains[c][step], *places[c], landings[c]) for c in range(2)
        ]
    for place, size in places:
        rows = pl.ds(pl.multiple_of(place, 8), size)
        full[rows, :] = tab[rows, :] * factor
    for step in (2, 1, 0):
        firsts = [gather_start(chains[c][step], *places[c]) for c in range(2)]
        split = min(middle + middle // 2 + 1, ny)
        if step == 1:
            for copy in cold_copies(middle):
                copy.start()
            cold_range(middle + 1, split)
        if step == 0:
            cold_range(split, ny)
        for c in range(2):
            gather_end(firsts[c], chains[c][step], *places[c])
        places = history[step]
    first = gather_start(core, *top)
    cold_range(middle, middle + 1)
    for h in range(HIGH):
        cold_out[h * own_low : (h + 1) * own_low, :] = cacc[:, h * width : (h + 1) * width]
    gather_end(first, core, *top)
    hot_out[...] = full[...]


def per_device(nx, ny, hot_ids, hot_grads, cold_grads, cold_slots, cold_counts):
    look, width = hot_grads.shape
    owners, capacity = cold_slots.shape[2], cold_slots.shape[3]
    px, py = 2 - nx % 2, 2 - ny % 2
    factor = (HOT / (look * nx * ny)) ** 0.5
    places = lax.broadcasted_iota(jnp.int32, (owners, capacity), 1)
    slots = jnp.where(places < cold_counts.reshape(owners, 1), cold_slots.reshape(owners, capacity), -1)
    cap_pieces = capacity // LANES
    slots = slots.reshape(owners, cap_pieces, LANES)
    pad = -cap_pieces % 8
    slots = jnp.pad(slots, ((0, 0), (0, pad), (0, 0)), constant_values=-1)
    ids = hot_ids.reshape(-1, 8, LANES)
    nxr, nyr = nx // px, ny // py
    s0 = HOT // px
    half = s0 // 2
    n_hot = 2 * ((px - 1) + 2 * ((nxr - 1) + (py - 1) + (nyr - 1)))

    def landing(n, rows):
        return pltpu.VMEM((max(n - 1, 1), rows // n, width), f32)

    f32 = jnp.float32
    hbm = pl.BlockSpec(memory_space=pltpu.HBM)
    vmem = pl.BlockSpec(memory_space=pltpu.VMEM)
    hot, cold = pl.pallas_call(
        functools.partial(kernel, nx, ny, factor, cap_pieces),
        out_shape=(
            jax.ShapeDtypeStruct((HOT, width), f32),
            jax.ShapeDtypeStruct((OWN_ROWS, width), f32),
        ),
        in_specs=[hbm, hbm, vmem, hbm],
        out_specs=(vmem, vmem),
        scratch_shapes=[
            pltpu.VMEM((HOT // HIGH, HIGH * width), f32),
            pltpu.VMEM((OWN_ROWS // HIGH, HIGH * width), f32),
            pltpu.VMEM((HOT, width), f32),
            pltpu.VMEM((HOT, width), f32),
            pltpu.VMEM((look, width), jnp.bfloat16),
            pltpu.VMEM(ids.shape, jnp.int32),
            pltpu.VMEM((owners, capacity, width), jnp.bfloat16),
            pltpu.VMEM((owners, cap_pieces + pad, LANES), jnp.int32),
            landing(px, HOT),
            landing(nxr, half),
            landing(py, half),
            landing(py, half // nxr),
            landing(nxr, half // py),
            landing(nyr, half // nxr // py),
            landing(nyr, half // nxr // py),
            pltpu.SemaphoreType.DMA((owners,)),
            pltpu.SemaphoreType.DMA((owners,)),
            pltpu.SemaphoreType.DMA((owners,)),
            pltpu.SemaphoreType.DMA((owners,)),
            pltpu.SemaphoreType.DMA((3,)),
            pltpu.SemaphoreType.DMA((n_hot,)),
            pltpu.SemaphoreType.DMA((n_hot,)),
        ],
        compiler_params=pltpu.CompilerParams(
            collective_id=0, has_side_effects=True, vmem_limit_bytes=63 * 1024 * 1024 - 1536 * 1024
        ),
    )(ids, hot_grads, slots, cold_grads.reshape(owners, capacity, width))
    return hot, cold.reshape(1, OWN_ROWS, width)


def solution(mesh):
    body = functools.partial(per_device, mesh.shape["gx"], mesh.shape["gy"])
    return jax.shard_map(
        body,
        mesh=mesh,
        in_specs=(
            P(("gx", "gy")),
            P(("gx", "gy"), None),
            P("gx", "gy", None, None, None),
            P("gx", "gy", None, None),
            P("gx", "gy", None),
        ),
        out_specs=(P(), P("gx", "gy", None)),
        check_vma=False,
    )
```

time: 59.9 us -> 56.1 us (0.937)
  Pallas kernels: 52 us -> 49.8 us
  local copies, waits for them, and re-layouts: 6.25 us -> 4.68 us
    pallas_call x1, Pallas kernels: 52 us -> 49.8 us  [per_device(): pl.pallas_call(functools.partial(kernel, nx, ny, factor, cap_pieces), out...]
    unnamed x8 -> x4, local copies, waits for them, and re-layouts: 5.51 us -> 3.32 us
    pad x1, local copies, waits for them, and re-layouts: 0.01 us -> 0.62 us  [per_device(): slots = jnp.pad(slots, ((0, 0), (0, pad), (0, 0)), constant_values=-1)]
where the time goes in v2:
time: 56.1 us; the launch traced here: 55.8 us
  Pallas kernels  49.8 us (89%)
  local copies, waits for them, and re-layouts  4.68 us (8%)
  other arithmetic  0.73 us (1%)
  between operations  0.65 us (1%)
    pallas_call x1, Pallas kernels, per_device(): pl.pallas_call(functools.partial(kernel, nx, ny, factor, cap_pieces), out...  49.8 us
    unnamed x4, local copies, waits for them, and re-layouts  3.32 us

profile of v2, /device:TPU:0, one launch (start us, length us, event | category | flops | bytes accessed | tf_op | source)
XLA Modules:
  0.0 55.8 jit_solution(14226897695305406013)
XLA Ops:
  0.6 0.7 %reshape.35 = s32[8,4,128]{2,1,0:T(4,128)S(1)} reshape(s32[1,1,8,512]{3,2,1,0:T(8,128)} %param.8) | data formatting | bytes 32768 | tf_op jit(solution)/shard_map/reshape | solution.py:233
  1.4 0.7 %compare_select_fusion = s32[8,4,128]{2,1,0:T(4,128)S(1)} fusion(s32[8,4,128]{2,1,0:T(4,128)S(1)} %reshape.35, s32[4,128]{1,0:T(4,128)S(1)} %multiply_add_fusion, s32[8]{0:T(128)} %bitcast.9), kind=kLoop, calls=%fused_computation | loop fusion | flops 8192 | bytes 34848 | tf_op jit(solution)/shard_map/jit(_where)/select_n | solution.py:233
  2.1 0.6 %pad.4.slots_ref = s32[8,8,128]{2,1,0:T(8,128)} pad(s32[8,4,128]{2,1,0:T(4,128)S(1)} %compare_select_fusion, s32[]{:T(128)} %constant.3.clone.1), padding=0_0x0_4x0_0 | pad | bytes 49156 | tf_op jit(solution)/shard_map/jit(_pad)/pad | solution.py:237
  2.7 49.8 %shard_map.68 = (f32[2048,128]{1,0:T(8,128)}, f32[2048,128]{1,0:T(8,128)}) custom-call(s32[8,8,128]{2,1,0:T(8,128)} %bitcast.8, bf16[8192,128]{1,0:T(8,128)(2,1)} %hot_ref.1, s32[8,8,128]{2,1,0:T(8,128)} %pad.4.slots_ref, bf16[8,512,128]{2,1,0:T(8,128)(2,1)} %bitcast.6), custom_call_target="tpu_custom_call" | custom-call | tf_op jit(solution)/shard_map/pallas_call | solution.py:250
  52.5 0.0 copy-start
  52.5 2.4 %copy.9 = f32[2048,128]{1,0:T(8,128)} copy(f32[2048,128]{1,0:T(8,128)} %get-tuple-element.8) | data formatting | bytes 2097152
  54.9 0.0 copy-done
  54.9 1.0 %copy.10 = f32[1,2048,128]{2,1,0:T(8,128)} copy(f32[1,2048,128]{2,1,0:T(8,128)S(1)} %bitcast.7) | data formatting | bytes 2097152
  (1 shorter events, 0.0 us)
Async XLA Ops:
  52.5 2.4 %copy-start = (f32[2048,128]{1,0:T(8,128)S(1)}, f32[2048,128]{1,0:T(8,128)}, u32[]{:S(2)}) copy-start(f32[2048,128]{1,0:T(8,128)} %get-tuple-element.5) | copy-start | bytes 3145732

commit v3 on v2

--- a/solution.py
+++ b/solution.py
@@ -194,10 +194,6 @@
         pending = [
             scatter_start(chains[c][step], *places[c], landings[c]) for c in range(2)
         ]
-        if step == 1:
-            cold_range(1, middle // 2 + 1)
-        if step == 2:
-            cold_range(middle // 2 + 1, middle)
         places = [
             scatter_end(pending[c], chains[c][step], *places[c], landings[c]) for c in range(2)
         ]
@@ -206,13 +202,12 @@
         full[rows, :] = tab[rows, :] * factor
     for step in (2, 1, 0):
         firsts = [gather_start(chains[c][step], *places[c]) for c in range(2)]
-        split = min(middle + middle // 2 + 1, ny)
         if step == 1:
             for copy in cold_copies(middle):
                 copy.start()
-            cold_range(middle + 1, split)
+            cold_range(1, middle)
         if step == 0:
-            cold_range(split, ny)
+            cold_range(middle + 1, ny)
         for c in range(2):
             gather_end(firsts[c], chains[c][step], *places[c])
         places = history[step]

time: 56.1 us -> 56.1 us (level)
  no operation moved by 1% of the time
where the time goes in v3:
time: 56.1 us; the launch traced here: 55.8 us
  Pallas kernels  49.8 us (89%)
  local copies, waits for them, and re-layouts  4.68 us (8%)
  other arithmetic  0.73 us (1%)
  between operations  0.65 us (1%)
    pallas_call x1, Pallas kernels, per_device(): pl.pallas_call(functools.partial(kernel, nx, ny, factor, cap_pieces), out...  49.8 us
    unnamed x4, local copies, waits for them, and re-layouts  3.32 us

profile of v3, /device:TPU:0, one launch (start us, length us, event | category | flops | bytes accessed | tf_op | source)
XLA Modules:
  0.0 55.8 jit_solution(6939670761675025125)
XLA Ops:
  0.6 0.7 %reshape.35 = s32[8,4,128]{2,1,0:T(4,128)S(1)} reshape(s32[1,1,8,512]{3,2,1,0:T(8,128)} %param.8) | data formatting | bytes 32768 | tf_op jit(solution)/shard_map/reshape | solution.py:228
  1.4 0.7 %compare_select_fusion = s32[8,4,128]{2,1,0:T(4,128)S(1)} fusion(s32[8,4,128]{2,1,0:T(4,128)S(1)} %reshape.35, s32[4,128]{1,0:T(4,128)S(1)} %multiply_add_fusion, s32[8]{0:T(128)} %bitcast.9), kind=kLoop, calls=%fused_computation | loop fusion | flops 8192 | bytes 34848 | tf_op jit(solution)/shard_map/jit(_where)/select_n | solution.py:228
  2.1 0.6 %pad.4.slots_ref = s32[8,8,128]{2,1,0:T(8,128)} pad(s32[8,4,128]{2,1,0:T(4,128)S(1)} %compare_select_fusion, s32[]{:T(128)} %constant.3.clone.1), padding=0_0x0_4x0_0 | pad | bytes 49156 | tf_op jit(solution)/shard_map/jit(_pad)/pad | solution.py:232
  2.7 49.8 %shard_map.68 = (f32[2048,128]{1,0:T(8,128)}, f32[2048,128]{1,0:T(8,128)}) custom-call(s32[8,8,128]{2,1,0:T(8,128)} %bitcast.8, bf16[8192,128]{1,0:T(8,128)(2,1)} %hot_ref.1, s32[8,8,128]{2,1,0:T(8,128)} %pad.4.slots_ref, bf16[8,512,128]{2,1,0:T(8,128)(2,1)} %bitcast.6), custom_call_target="tpu_custom_call" | custom-call | tf_op jit(solution)/shard_map/pallas_call | solution.py:245
  52.5 0.0 copy-start
  52.5 2.4 %copy.9 = f32[2048,128]{1,0:T(8,128)} copy(f32[2048,128]{1,0:T(8,128)} %get-tuple-element.8) | data formatting | bytes 2097152
  54.9 0.0 copy-done
  54.9 1.0 %copy.10 = f32[1,2048,128]{2,1,0:T(8,128)} copy(f32[1,2048,128]{2,1,0:T(8,128)S(1)} %bitcast.7) | data formatting | bytes 2097152
  (1 shorter events, 0.0 us)
Async XLA Ops:
  52.5 2.4 %copy-start = (f32[2048,128]{1,0:T(8,128)S(1)}, f32[2048,128]{1,0:T(8,128)}, u32[]{:S(2)}) copy-start(f32[2048,128]{1,0:T(8,128)} %get-tuple-element.5) | copy-start | bytes 3145732
